TPU v7x, 32 devices: a whole 2x2x4 slice. The times are simulated.
32 devices in a mesh: replica: 4 (over z), tensor: 8 (over y, x, core).
Axes of the slice: x: 2, y: 2, z: 4, core: 2. Of those that a mesh axis runs over, the one named last changes fastest.
Arguments:
- hidden_in: bfloat16 [4, 64, 8192], P(None, 'replica'), may hold values from -96 to 96
- norm_gain: bfloat16 [8192], replicated, may hold values from 0.25 to 1.75
- query_weight: bfloat16 [8192, 8192], P(None, 'tensor'), may hold values from -0.0625 to 0.0625
- w_keyvalue: bfloat16 [8192, 2048], P(None, 'tensor'), may hold values from -0.0625 to 0.0625
- output_weight: bfloat16 [8192, 8192], P('tensor'), may hold values from -0.0625 to 0.0625
- query_down_factor: bfloat16 [64, 8192], P(None, ('replica', 'tensor')), may hold values from -0.0625 to 0.0625
- query_up_factor: bfloat16 [64, 8192], P(None, ('replica', 'tensor')), may hold values from -0.75 to 0.75
- output_down_factor: bfloat16 [64, 8192], P(None, ('replica', 'tensor')), may hold values from -0.0625 to 0.0625
- output_up_factor: bfloat16 [64, 8192], P(None, ('replica', 'tensor')), may hold values from -0.75 to 0.75
- keys_cache: bfloat16 [16, 32, 1024, 128], P('tensor', 'replica'), may hold values from -250 to 250
- values_cache: bfloat16 [16, 32, 1024, 128], P('tensor', 'replica'), may hold values from -5 to 5
- cache_lengths: int32 [64], P('replica'), may hold values from 256 to 1024, as said below
Outputs:
- attended: bfloat16 [4, 64, 8192], P(None, 'replica', 'tensor')
Inputs may be any that keep to these rules, and one draw needn't show every extreme that they name: `cache_lengths`: some row holds exactly 1024 positions and some other row exactly 256.
All inputs are finite; a program needn't handle non-finite values.
Results may differ from a plain program's by a relative error of at most 0.018.
Values may be sent and summed in bfloat16 or wider, within the bound.
No kernel may reach another device: no remote copies, remote signals or barrier semaphores. Data moves between devices by JAX's collectives and lax.ppermute only.
A program may use at most 128 MiB of HBM per device.

v0:
```python
import math
import jax
import jax.numpy as jnp
from jax import lax
from jax.sharding import PartitionSpec as P

HQ = 64
KVH = 8
HD = 128
CAP = 1024
adapter_scale = 2.0
rope_base = 1000000.0
norm_epsilon = 1e-06


def swapped(array, axis, apart):
    return lax.ppermute(array, axis, [(i, i ^ 1 << apart) for i in range(lax.axis_size(axis))])


def for_sending(array):
    return jax.tree.map(lambda a: a.astype(jnp.bfloat16) if a.dtype == jnp.float32 else a, array)


def rms_norm(hidden, norm_gain):
    values = hidden.astype(jnp.float32)
    mean_square = jnp.mean(values * values, axis=-1, keepdims=True)
    return values * lax.rsqrt(mean_square + norm_epsilon) * norm_gain.astype(jnp.float32)


def apply_rotary(vectors, positions):
    half_width = vectors.shape[-1] // 2
    exponents = jnp.arange(half_width, dtype=jnp.float32) * (2.0 / vectors.shape[-1])
    frequency = jnp.power(rope_base, -exponents)
    angles = positions.astype(jnp.float32)[:, None, None] * frequency
    cosine_values = jnp.cos(angles)
    sine_values = jnp.sin(angles)
    leading = vectors[..., :half_width]
    trailing = vectors[..., half_width:]
    return jnp.concatenate(
        [
            leading * cosine_values - trailing * sine_values,
            trailing * cosine_values + leading * sine_values,
        ],
        axis=-1,
    )


def attend_block(queries, cache_keys, cache_values, lengths, fresh_keys, fresh_values):
    inverse_root = 1.0 / math.sqrt(queries.shape[-1])
    cached = (
        jnp.einsum("ngd,npd->ngp", queries, cache_keys, preferred_element_type=jnp.float32)
        * inverse_root
    )
    visible = jnp.arange(cache_keys.shape[1])[None, :] < lengths[:, None]
    cached = jnp.where(visible[:, None, :], cached, -jnp.inf)
    recent = (
        jnp.einsum("ngd,nsd->ngs", queries, fresh_keys, preferred_element_type=jnp.float32)
        * inverse_root
    )
    highest = jnp.maximum(
        jnp.max(cached, axis=-1, keepdims=True), jnp.max(recent, axis=-1, keepdims=True)
    )
    cached_exp = jnp.exp(cached - highest)
    recent_exp = jnp.exp(recent - highest)
    denominator = jnp.sum(cached_exp, axis=-1, keepdims=True) + jnp.sum(
        recent_exp, axis=-1, keepdims=True
    )
    cached_weight = (cached_exp / denominator).astype(jnp.bfloat16)
    recent_weight = (recent_exp / denominator).astype(jnp.bfloat16)
    combined = jnp.einsum(
        "ngp,npd->ngd", cached_weight, cache_values, preferred_element_type=jnp.float32
    )
    combined = combined + jnp.einsum(
        "ngs,nsd->ngd", recent_weight, fresh_values, preferred_element_type=jnp.float32
    )
    return combined.astype(jnp.bfloat16)


def rank_contraction(left_factor, right_factor):
    return lax.dot_general(
        left_factor, right_factor, (((0,), (0,)), ((), ())), preferred_element_type=jnp.float32
    )


def pick_half(paired, lower_half):
    return jnp.where(lower_half, paired[:, 0], paired[:, 1])


def pick_middle(paired, lower_half):
    return jnp.where(lower_half, paired[:, :, 0], paired[:, :, 1])


def shards(
    hidden_in,
    norm_gain,
    query_weight,
    w_keyvalue,
    output_weight,
    query_down_factor,
    query_up_factor,
    output_down_factor,
    output_up_factor,
    keys_cache,
    values_cache,
    cache_lengths,
):
    tensor_index = lax.axis_index("tensor")
    slice_width = query_weight.shape[1]
    complete_down_factor, complete_up_factor, wide_up, wide_down = (
        lax.all_gather(query_down_factor, ("replica", "tensor"), axis=1, tiled=True),
        lax.all_gather(output_up_factor, ("replica", "tensor"), axis=1, tiled=True),
        lax.all_gather(query_up_factor, ("replica", "tensor"), axis=1, tiled=True),
        lax.all_gather(output_down_factor, ("replica", "tensor"), axis=1, tiled=True),
    )
    query_weight_slice = lax.dynamic_slice_in_dim(
        wide_up, tensor_index * slice_width, slice_width, 1
    )
    output_weight_slice = lax.dynamic_slice_in_dim(
        wide_down, tensor_index * slice_width, slice_width, 1
    )
    query_merged_weight = (
        query_weight.astype(jnp.float32)
        + adapter_scale * rank_contraction(complete_down_factor, query_weight_slice)
    ).astype(jnp.bfloat16)
    output_merged_weight = (
        output_weight.astype(jnp.float32)
        + adapter_scale * rank_contraction(output_weight_slice, complete_up_factor)
    ).astype(jnp.bfloat16)
    rows_local = hidden_in.shape[1]
    rows_half = rows_local // 2
    heads_local = slice_width // HD
    group_size = HQ // KVH
    entries = keys_cache.shape[0]
    lower_half = tensor_index % 2 == 0
    groups_local = max(heads_local // group_size, 1)
    block_count = groups_local * 2 * rows_half
    if entries == 1:
        own_lengths = pick_half(cache_lengths.reshape(rows_half, 2), lower_half)
        own_keys = keys_cache[0]
        own_values = values_cache[0]
    else:
        own_lengths = jnp.tile(cache_lengths.reshape(rows_half, 2).T, (groups_local, 1)).reshape(
            block_count
        )
        own_keys = keys_cache.reshape(block_count, CAP, HD)
        own_values = values_cache.reshape(block_count, CAP, HD)
    step_count = hidden_in.shape[0]
    normed_all = (
        rms_norm(hidden_in, norm_gain)
        .astype(jnp.bfloat16)
        .reshape(step_count * rows_local, hidden_in.shape[2])
    )
    positions_all = (
        cache_lengths[None, :] + jnp.arange(step_count, dtype=jnp.int32)[:, None]
    ).reshape(step_count * rows_local)
    queries_all = jnp.dot(
        normed_all, query_merged_weight, preferred_element_type=jnp.float32
    ).reshape(step_count * rows_local, heads_local, HD)
    queries_all = apply_rotary(queries_all, positions_all).astype(jnp.bfloat16)
    projected_all = jnp.dot(normed_all, w_keyvalue, preferred_element_type=jnp.float32)
    heads_list = []
    if entries == 1:
        rotated_all = apply_rotary(projected_all[:, None, :], positions_all)[:, 0]
        projected_all = jnp.where(lower_half, rotated_all, projected_all).astype(jnp.bfloat16)
        query_pairs = queries_all.reshape(step_count, rows_half, 2, heads_local, HD)
        projected_pairs = projected_all.reshape(step_count, rows_half, 2, HD)
        own_queries = pick_middle(query_pairs, lower_half)
        other_queries = pick_middle(query_pairs, jnp.logical_not(lower_half))
        own_projected = pick_middle(projected_pairs, lower_half)
        other_projected = pick_middle(projected_pairs, jnp.logical_not(lower_half))
        outgoing = jnp.concatenate(
            [other_queries.reshape(step_count, rows_half, heads_local * HD), other_projected],
            axis=2,
        )
        incoming = swapped(outgoing, "tensor", 0)
        partner_queries = incoming[:, :, : heads_local * HD].reshape(
            step_count, rows_half, heads_local, HD
        )
        partner_projected = incoming[:, :, heads_local * HD :]
        group_queries_all = jnp.where(
            lower_half,
            jnp.concatenate([own_queries, partner_queries], axis=2),
            jnp.concatenate([partner_queries, own_queries], axis=2),
        )
        keys_steps = jnp.where(lower_half, own_projected, partner_projected).transpose(1, 0, 2)
        values_steps = jnp.where(lower_half, partner_projected, own_projected).transpose(1, 0, 2)
        kept_list = []
        sent_list = []
        for decode_step in range(step_count):
            attended_heads = attend_block(
                group_queries_all[decode_step],
                own_keys,
                own_values,
                own_lengths,
                keys_steps[:, : decode_step + 1],
                values_steps[:, : decode_step + 1],
            )
            first_heads = attended_heads[:, :heads_local]
            second_heads = attended_heads[:, heads_local:]
            kept_list.append(
                jnp.where(lower_half, first_heads, second_heads).reshape(
                    rows_half, heads_local * HD
                )
            )
            sent_list.append(
                jnp.where(lower_half, second_heads, first_heads).reshape(
                    rows_half, heads_local * HD
                )
            )
        kept_all = jnp.stack(kept_list)
        returned_all = swapped(for_sending(jnp.stack(sent_list)), "tensor", 0)
        rows_first = jnp.where(lower_half, kept_all, returned_all)
        rows_second = jnp.where(lower_half, returned_all, kept_all)
        heads_stacked = jnp.stack([rows_first, rows_second], axis=2).reshape(
            step_count * rows_local, heads_local * HD
        )
    else:
        keyvals = projected_all.reshape(step_count, rows_local, groups_local, 2, HD)
        new_keys = apply_rotary(
            keyvals[:, :, :, 0].reshape(step_count * rows_local, groups_local, HD), positions_all
        ).astype(jnp.bfloat16)
        new_values = keyvals[:, :, :, 1].astype(jnp.bfloat16)
        keys_steps = (
            new_keys.reshape(step_count, rows_half, 2, groups_local, HD)
            .transpose(3, 2, 1, 0, 4)
            .reshape(block_count, step_count, HD)
        )
        values_steps = (
            new_values.reshape(step_count, rows_half, 2, groups_local, HD)
            .transpose(3, 2, 1, 0, 4)
            .reshape(block_count, step_count, HD)
        )
        group_queries_all = (
            queries_all.reshape(step_count, rows_half, 2, groups_local, group_size, HD)
            .transpose(0, 3, 2, 1, 4, 5)
            .reshape(step_count, block_count, group_size, HD)
        )
        for decode_step in range(step_count):
            attended_heads = attend_block(
                group_queries_all[decode_step],
                own_keys,
                own_values,
                own_lengths,
                keys_steps[:, : decode_step + 1],
                values_steps[:, : decode_step + 1],
            )
            heads_list.append(
                attended_heads.reshape(groups_local, 2, rows_half, group_size, HD)
                .transpose(2, 1, 0, 3, 4)
                .reshape(rows_local, heads_local * HD)
            )
        heads_stacked = jnp.stack(heads_list).reshape(step_count * rows_local, heads_local * HD)
    partial_all = jnp.dot(heads_stacked, output_merged_weight, preferred_element_type=jnp.float32)
    shares_all = lax.psum_scatter(
        partial_all.astype(jnp.bfloat16), "tensor", scatter_dimension=1, tiled=True
    ).astype(jnp.float32)
    return shares_all.reshape(step_count, rows_local, shares_all.shape[1]).astype(jnp.bfloat16)


def solution(mesh):
    return jax.shard_map(
        shards,
        mesh=mesh,
        in_specs=(
            P(None, "replica", None),
            P(),
            P(None, "tensor"),
            P(None, "tensor"),
            P("tensor", None),
            P(None, ("replica", "tensor")),
            P(None, ("replica", "tensor")),
            P(None, ("replica", "tensor")),
            P(None, ("replica", "tensor")),
            P("tensor", "replica", None, None),
            P("tensor", "replica", None, None),
            P("replica"),
        ),
        out_specs=P(None, "replica", "tensor"),
        check_vma=False,
    )
```

profile of v0, /device:TPU:0, one launch (start us, length us, event | category | flops | bytes accessed | tf_op | source)
XLA Modules:
  0.0 284.2 jit_solution(3601060914490597169)
XLA Ops:
  6.5 0.7 all-gather.5.cloned.1.call-update
  7.3 0.7 all-gather.7.cloned.1.call-update
  8.1 0.7 all-gather.11.cloned.1.call-update
  8.8 0.5 all-gather.9.cloned.1.call-update
  9.4 0.7 add_convert_fusion.5
  10.0 0.7 reshape.366
  10.8 0.7 convert_element_type.109
  11.5 1.5 fusion.6
  13.0 6.5 %copy.40 = bf16[256,8192]{1,0:T(8,128)(2,1)} copy(bf16[256,8192]{0,1:T(8,128)(2,1)} %bitcast.116) | data formatting | bytes 8388608 | tf_op jit(solution)/shard_map/reshape.133
  19.5 0.3 fusion.8
  19.8 4.0 %convolution_bitcast_fusion = f32[4,16,1,2,128]{4,1,3,0,2:T(8,128)S(1)} fusion(bf16[2,128,8192,1]{2,1,0,3:T(8,128)(2,1)} %bitcast.117, bf16[4,16,8192]{2,1,0:T(8,128)(2,1)S(1)} %fusion.8), kind=kOutput, calls=%fused_computation.23 | convolution fusion | flops 268435456 | bytes 5308416 | tf_op jit(solution)/shard_map/dot_general | solution.py:160
  23.9 20.9 %copy.24 = bf16[8192,1024]{0,1:T(8,128)(2,1)} copy(bf16[8192,1024]{1,0:T(8,128)(2,1)} %param.14) | data formatting | bytes 33554432 | tf_op args[2]
  44.8 0.1 convert_element_type.114
  44.9 0.2 multiply_cosine_fusion.1
  45.1 0.2 fusion.41
  45.4 0.1 lt.15
  45.5 0.1 iota_compare_fusion
  45.6 0.1 pad_maximum_fusion.1
  45.7 19.6 %all-gather.5.cloned.1.call-done = bf16[64,8192]{1,0:T(8,128)(2,1)} async-done(((bf16[64,256]{1,0:T(8,128)(2,1)}), bf16[64,8192]{1,0:T(8,128)(2,1)}) %all-gather.5.cloned.1.call-update) | async-done | bytes 1048592 | tf_op jit(solution)/shard_map/all_gather | solution.py:112
  65.3 54.9 %all-gather.7.cloned.1.call-done = bf16[64,8192]{1,0:T(8,128)(2,1)} async-done(((bf16[64,256]{1,0:T(8,128)(2,1)}), bf16[64,8192]{1,0:T(8,128)(2,1)}) %all-gather.7.cloned.1.call-update) | async-done | bytes 1048592 | tf_op jit(solution)/shard_map/all_gather | solution.py:110
  120.1 11.8 %fusion = bf16[8192,1024]{0,1:T(8,128)(2,1)} fusion(bf16[8192,1024]{0,1:T(8,128)(2,1)} %copy.24, bf16[64,8192]{1,0:T(8,128)(2,1)} %all-gather.7.cloned.1.call-done, bf16[64,8192]{1,0:T(8,128)(2,1)} %all-gather.5.cloned.1.call-done, s32[]{:T(128)S(6)} %select_n.17), kind=kOutput, calls=%fused_computation.1 | convolution fusion | flops 1107296256 | bytes 34734084 | tf_op jit(solution)/shard_map/dot_general | solution.py:80
  131.9 9.3 %fusion.72 = f32[64,8,128]{2,0,1:T(8,128)S(1)} fusion(bf16[64,8192,1]{1,0,2:T(8,128)(2,1)} %bitcast.115, bf16[8,128,8192]{2,1,0:T(8,128)(2,1)} %bitcast.106), kind=kOutput, calls=%fused_computation.122 | convolution fusion | flops 1073741824 | bytes 18087936 | tf_op jit(solution)/shard_map/dot_general | solution.py:156
  141.2 0.1 subtract_convert_fusion
  141.4 0.4 maximum_bitcast_fusion
  141.7 0.1 fusion.64
  141.9 0.1 fusion.57
  142.0 0.2 fusion.70
  142.2 1.3 fusion.71
  143.4 2.0 fusion.69
  145.5 0.2 fusion.68
  145.6 1.3 fusion.67
  146.9 0.2 fusion.18
  147.2 0.7 fusion.16
  148.0 0.2 fusion.19
  148.2 2.9 %fusion.22 = f32[16,8,128]{2,1,0:T(8,128)S(1)} fusion(bf16[16,1024,128]{2,1,0:T(8,128)(2,1)} %bitcast.111, f32[16,8,1024]{2,1,0:T(8,128)S(1)} %copy-done.3, f32[16,8]{1,0:T(8,128)S(1)} %add.101, f32[16,8]{1,0:T(8,128)S(1)} %max.31), kind=kOutput, calls=%fused_computation.45 | convolution fusion | flops 33947648 | bytes 4785152 | tf_op jit(solution)/shard_map/ngp,npd->ngd/dot_general | solution.py:70
  151.1 0.2 fusion.13
  151.4 0.2 fusion.20
  151.7 2.9 %fusion.23 = f32[16,8,128]{2,1,0:T(8,128)S(1)} fusion(bf16[16,1024,128]{2,1,0:T(8,128)(2,1)} %bitcast.112, f32[16,8,1024]{2,1,0:T(8,128)S(1)} %get-tuple-element.22, f32[16,8]{1,0:T(8,128)S(1)} %add.103, f32[16,8]{1,0:T(8,128)S(1)} %max.32), kind=kOutput, calls=%fused_computation.46 | convolution fusion | flops 33947648 | bytes 4785152 | tf_op jit(solution)/shard_map/ngp,npd->ngd/dot_general | solution.py:70
  154.6 0.2 fusion.14
  154.9 0.2 fusion.66
  155.1 3.6 %fusion.65 = (f32[16,8]{1,0:T(8,128)S(1)}, f32[16,8,1024]{2,1,0:T(8,128)S(1)}) fusion(bf16[16,8,128]{2,1,0:T(8,128)(2,1)S(1)} %bitcast.121, bf16[16,1024,128]{2,1,0:T(8,128)(2,1)} %bitcast.107, pred[16,1024]{1,0:T(8,128)(4,1)S(1)} %iota_compare_fusion), kind=kOutput, calls=%fused_computation.115 | convolution fusion | flops 33947520 | bytes 4768256 | tf_op jit(solution)/shard_map/ngd,npd->ngp/dot_general | solution.py:51
  158.7 0.2 fusion.21
  159.0 0.7 fusion.24
  159.7 0.2 fusion.15
  160.0 15.2 %all-gather.11.cloned.1.call-done = bf16[64,8192]{1,0:T(8,128)(2,1)} async-done(((bf16[64,256]{1,0:T(8,128)(2,1)}), bf16[64,8192]{1,0:T(8,128)(2,1)}) %all-gather.11.cloned.1.call-update) | async-done | bytes 1048592 | tf_op jit(solution)/shard_map/all_gather | solution.py:111
  175.1 54.7 %all-gather.9.cloned.1.call-done = bf16[64,8192]{1,0:T(8,128)(2,1)} async-done(((bf16[64,256]{1,0:T(8,128)(2,1)}), bf16[64,8192]{1,0:T(8,128)(2,1)}) %all-gather.9.cloned.1.call-update) | async-done | bytes 1048592 | tf_op jit(solution)/shard_map/all_gather | solution.py:113
  229.9 12.0 %fusion.5 = bf16[64,8192]{1,0:T(8,128)(2,1)} fusion(bf16[64,1024]{1,0:T(8,128)(2,1)S(1)} %bitcast.130, bf16[1024,8192]{1,0:T(8,128)(2,1)} %param.16, bf16[64,8192]{1,0:T(8,128)(2,1)} %all-gather.11.cloned.1.call-done, bf16[64,8192]{1,0:T(8,128)(2,1)} %all-gather.9.cloned.1.call-done, s32[]{:T(128)S(6)} %select_n.17), kind=kOutput, calls=%fused_computation.6 | convolution fusion | flops 2181562368 | bytes 19136516 | tf_op jit(solution)/shard_map/dot_general | solution.py:253
  241.9 35.8 %reduce-scatter.2.cloned.1.call-done = bf16[64,1024]{1,0:T(8,128)(2,1)} async-done(((bf16[64,8192]{1,0:T(8,128)(2,1)}), bf16[64,1024]{1,0:T(8,128)(2,1)}) %reduce-scatter.2.cloned.1.call-update) | async-done | bytes 131088 | tf_op jit(solution)/shard_map/reduce_scatter | solution.py:254
  (51 shorter events, 0.7 us)
Async XLA Ops:
  6.5 58.7 %all-gather.5.cloned.1.call-start = ((), (), s32[]{:S(2)}) async-start(), calls=%async_computation.1 | async-start | bytes 1081344 | tf_op jit(solution)/shard_map/all_gather | solution.py:112
  7.3 112.9 %all-gather.7.cloned.1.call-start = ((), (), s32[]{:S(2)}) async-start(), calls=%async_computation.2 | async-start | bytes 1081344 | tf_op jit(solution)/shard_map/all_gather | solution.py:110
  8.0 167.1 %all-gather.11.cloned.1.call-start = ((), (), s32[]{:S(2)}) async-start(), calls=%async_computation.4 | async-start | bytes 1081344 | tf_op jit(solution)/shard_map/all_gather | solution.py:111
  8.7 221.2 %all-gather.9.cloned.1.call-start = ((), (), s32[]{:S(2)}) async-start(), calls=%async_computation.3 | async-start | bytes 1081344 | tf_op jit(solution)/shard_map/all_gather | solution.py:113
  9.3 268.4 %reduce-scatter.2.cloned.1.call-start = ((), (), s32[]{:S(2)}) async-start(), calls=%async_computation.5 | async-start | bytes 1179648 | tf_op jit(solution)/shard_map/reduce_scatter | solution.py:254
  13.0 6.5 %copy-start.5 = (bf16[4,16,8192]{2,1,0:T(8,128)(2,1)S(1)}, bf16[4,16,8192]{2,1,0:T(8,128)(2,1)}, u32[]{:S(2)}) copy-start(bf16[4,16,8192]{2,1,0:T(8,128)(2,1)} %param.12) | copy-start | bytes 3145732
  19.8 25.0 %copy-start.4 = (bf16[4,16,8192]{2,1,0:T(8,128)(2,1)}, bf16[4,16,8192]{2,1,0:T(8,128)(2,1)S(1)}, u32[]{:S(2)}) copy-start(bf16[4,16,8192]{2,1,0:T(8,128)(2,1)S(1)} %fusion.8) | copy-start | bytes 3145732
  131.9 10.3 %copy-start = (bf16[2,8,1024,128]{3,2,1,0:T(8,128)(2,1)S(1)}, bf16[2,8,1024,128]{3,2,1,0:T(8,128)(2,1)}, u32[]{:S(2)}) copy-start(bf16[2,8,1024,128]{3,2,1,0:T(8,128)(2,1)} %param.21) | copy-start | bytes 12582916
  143.4 3.7 %copy-start.1 = (bf16[2,8,1024,128]{3,2,1,0:T(8,128)(2,1)S(1)}, bf16[2,8,1024,128]{3,2,1,0:T(8,128)(2,1)}, u32[]{:S(2)}) copy-start(bf16[2,8,1024,128]{3,2,1,0:T(8,128)(2,1)} %param.22) | copy-start | bytes 12582916
  146.9 1.1 copy-start.3
  154.9 4.1 %copy-start.2 = (bf16[2,8,1024,128]{3,2,1,0:T(8,128)(2,1)S(1)}, bf16[2,8,1024,128]{3,2,1,0:T(8,128)(2,1)}, u32[]{:S(2)}) copy-start(bf16[2,8,1024,128]{3,2,1,0:T(8,128)(2,1)} %param.22) | copy-start | bytes 12582916
Sparse Core Ops, SparseCore 0:
  10.2 55.0 all-gather.4
  68.1 51.9 all-gather.6
  123.0 52.0 all-gather.10
  177.9 51.9 all-gather.8
  242.0 35.6 reduce-scatter.1
where the time goes:
time: 285 us; the launch traced here: 284 us
  waiting for transfers between devices  183 us (64%)
  matrix products  53.7 us (19%)
  local copies, waits for them, and re-layouts  28.7 us (10%)
  between operations  13.5 us (5%)
  other arithmetic  5.41 us (2%)
    all_gather x1, waiting for transfers between devices, shards(): lax.all_gather(query_down_factor, ('replica', 'tensor'), axis=1, tiled=True)  54.9 us
    all_gather x1, waiting for transfers between devices, shards(): lax.all_gather(output_down_factor, ('replica', 'tensor'), axis=1, tiled=T...  54.7 us
    reduce_scatter x1, waiting for transfers between devices, shards(): lax.psum_scatter(partial_all.astype(jnp.bfloat16), 'tensor', scatter_dime...  35.8 us
    unnamed x13, local copies, waits for them, and re-layouts  21 us
    all_gather x1, waiting for transfers between devices, shards(): lax.all_gather(query_up_factor, ('replica', 'tensor'), axis=1, tiled=True)  19.6 us
    all_gather x1, waiting for transfers between devices, shards(): lax.all_gather(output_up_factor, ('replica', 'tensor'), axis=1, tiled=True)  15.2 us
    dot_general x1, matrix products, shards(): jnp.dot(heads_stacked, output_merged_weight, preferred_element_type=jnp.f...  12 us
    dot_general x1, matrix products, rank_contraction(): lax.dot_general(left_factor, right_factor, (((0,), (0,)), ((), ())), pref...  11.8 us
  transfers between devices with their start and end apart: 5, of which 5 were waited for; matrix products, arithmetic and copies ran while one was open for 27% of the time, Pallas kernels for 0%

commit v1 on v0

--- a/solution.py
+++ b/solution.py
@@ -11,6 +11,18 @@
 adapter_scale = 2.0
 rope_base = 1000000.0
 norm_epsilon = 1e-06
+
+
+def gather_by_bits(x, axis, dim):
+    ways, here, step = (lax.axis_size(axis), lax.axis_index(axis), x.shape[dim])
+    line, have = (x, 1)
+    while have < ways:
+        line = jnp.concatenate(
+            [line, lax.ppermute(line, axis, [(d, (d - have) % ways) for d in range(ways)])],
+            axis=dim,
+        )
+        have = 2 * have
+    return jnp.roll(line, here * step, axis=dim)
 
 
 def swapped(array, axis, apart):
@@ -109,7 +121,7 @@
     complete_down_factor, complete_up_factor, wide_up, wide_down = (
         lax.all_gather(query_down_factor, ("replica", "tensor"), axis=1, tiled=True),
         lax.all_gather(output_up_factor, ("replica", "tensor"), axis=1, tiled=True),
-        lax.all_gather(query_up_factor, ("replica", "tensor"), axis=1, tiled=True),
+        gather_by_bits(query_up_factor, ("replica", "tensor"), 1),
         lax.all_gather(output_down_factor, ("replica", "tensor"), axis=1, tiled=True),
     )
     query_weight_slice = lax.dynamic_slice_in_dim(

time: 285 us -> 242 us (0.85)
  waiting for transfers between devices: 183 us -> 123 us
  starting transfers between devices: 0.15 us -> 8.91 us
  local copies, waits for them, and re-layouts: 28.7 us -> 36.4 us
    all_gather x1, waiting for transfers between devices: 54.9 us -> 0.01 us  [shards(): lax.all_gather(query_down_factor, ('replica', 'tensor'), axis=1, tiled=True)]
    all_gather x1, waiting for transfers between devices: 54.7 us -> 0.02 us  [shards(): lax.all_gather(output_down_factor, ('replica', 'tensor'), axis=1, tiled=T...]
    all_gather x1, waiting for transfers between devices: 15.2 us -> 55.2 us  [shards(): lax.all_gather(output_up_factor, ('replica', 'tensor'), axis=1, tiled=True)]
    ppermute x0 -> x5, waiting for transfers between devices: none -> 31 us  [gather_by_bits(): lax.ppermute(line, axis, [(d, (d - have) % ways) for d in range(ways)])]
    all_gather x1 -> x0, waiting for transfers between devices: 19.6 us -> none  [shards(): lax.all_gather(query_up_factor, ('replica', 'tensor'), axis=1, tiled=True)]
    ppermute x0 -> x5, starting transfers between devices: none -> 8.79 us  [gather_by_bits(): lax.ppermute(line, axis, [(d, (d - have) % ways) for d in range(ways)])]
    unnamed x13 -> x27, local copies, waits for them, and re-layouts: 21 us -> 27.7 us
  transfers between devices with their start and end apart: 5 -> 9, of which waited for: 5 -> 5; matrix products, arithmetic and copies ran while one was open for 27% -> 35% of each run, Pallas kernels for 0% -> 0%
where the time goes in v1:
time: 242 us; the launch traced here: 241 us
  waiting for transfers between devices  123 us (51%)
  matrix products  53.6 us (22%)
  local copies, waits for them, and re-layouts  36.4 us (15%)
  between operations  13.6 us (6%)
  starting transfers between devices  8.91 us (4%)
  other arithmetic  5.44 us (2%)
    all_gather x1, waiting for transfers between devices, shards(): lax.all_gather(output_up_factor, ('replica', 'tensor'), axis=1, tiled=True)  55.2 us
    reduce_scatter x1, waiting for transfers between devices, shards(): lax.psum_scatter(partial_all.astype(jnp.bfloat16), 'tensor', scatter_dime...  35.8 us
    ppermute x5, waiting for transfers between devices, gather_by_bits(): lax.ppermute(line, axis, [(d, (d - have) % ways) for d in range(ways)])  31 us
    unnamed x27, local copies, waits for them, and re-layouts  27.7 us
    dot_general x1, matrix products, shards(): jnp.dot(heads_stacked, output_merged_weight, preferred_element_type=jnp.f...  12 us
    dot_general x1, matrix products, rank_contraction(): lax.dot_general(left_factor, right_factor, (((0,), (0,)), ((), ())), pref...  11.8 us
    dot_general x1, matrix products, shards(): jnp.dot(normed_all, query_merged_weight, preferred_element_type=jnp.float32)  9.1 us
    ppermute x5, starting transfers between devices, gather_by_bits(): lax.ppermute(line, axis, [(d, (d - have) % ways) for d in range(ways)])  8.79 us
  transfers between devices with their start and end apart: 9, of which 5 were waited for; matrix products, arithmetic and copies ran while one was open for 35% of the time, Pallas kernels for 0%

profile of v1, /device:TPU:0, one launch (start us, length us, event | category | flops | bytes accessed | tf_op | source)
XLA Modules:
  0.0 241.3 jit_solution(6305287586013553664)
XLA Ops:
  6.5 0.7 all-gather.4.cloned.1.call-update
  7.3 0.7 all-gather.6.cloned.1.call-update
  8.1 6.5 %collective-permute-start = (bf16[64,256]{1,0:T(8,128)(2,1)}, bf16[64,256]{1,0:T(8,128)(2,1)S(1)}, u32[]{:S(2)}, u32[]{:S(2)}) collective-permute-start(bf16[64,256]{1,0:T(8,128)(2,1)} %param.18), channel_id=1, source_target_pairs={{0,31},{1,0},{2,1},{3,2},{4,3},{5,4},{6,5},{7,6},{8,7},{9,8},{10,9... | collective-permute-start | bytes 98312 | tf_op jit(solution)/shard_map/ppermute | solution.py:21
  14.6 0.7 convert_element_type.109
  15.3 1.5 fusion.6
  16.8 0.7 add_convert_fusion.5
  17.5 6.5 %copy.40 = bf16[256,8192]{1,0:T(8,128)(2,1)} copy(bf16[256,8192]{0,1:T(8,128)(2,1)} %bitcast.116) | data formatting | bytes 8388608 | tf_op jit(solution)/shard_map/reshape.133
  24.0 0.3 fusion.8
  24.3 4.0 %convolution_bitcast_fusion = f32[4,16,1,2,128]{4,1,3,0,2:T(8,128)S(1)} fusion(bf16[2,128,8192,1]{2,1,0,3:T(8,128)(2,1)} %bitcast.117, bf16[4,16,8192]{2,1,0:T(8,128)(2,1)S(1)} %fusion.8), kind=kOutput, calls=%fused_computation.23 | convolution fusion | flops 268435456 | bytes 5308416 | tf_op jit(solution)/shard_map/dot_general | solution.py:172
  28.4 1.2 collective-permute-start.1
  30.1 2.6 %collective-permute-done.1 = bf16[64,512]{1,0:T(8,128)(2,1)S(1)} collective-permute-done((bf16[64,512]{1,0:T(8,128)(2,1)S(1)}, bf16[64,512]{1,0:T(8,128)(2,1)S(1)}, u32[]{:S(2)}, u32[]{:S(2)}) %collective-permute-start.1) | collective-permute-done | bytes 65568 | tf_op jit(solution)/shard_map/ppermute | solution.py:21
  32.8 0.6 collective-permute-start.2
  33.5 20.9 %copy.24 = bf16[8192,1024]{0,1:T(8,128)(2,1)} copy(bf16[8192,1024]{1,0:T(8,128)(2,1)} %param.14) | data formatting | bytes 33554432 | tf_op args[2]
  54.5 0.6 constant_dynamic-update-slice_fusion.4
  55.1 0.5 collective-permute-start.3
  55.6 0.6 constant_dynamic-update-slice_fusion.3
  56.3 0.7 constant_dynamic-update-slice_fusion.2
  56.9 0.7 constant_dynamic-update-slice_fusion.1
  57.6 7.8 %collective-permute-done.3 = bf16[64,2048]{1,0:T(8,128)(2,1)S(1)} collective-permute-done((bf16[64,2048]{1,0:T(8,128)(2,1)S(1)}, bf16[64,2048]{1,0:T(8,128)(2,1)S(1)}, u32[]{:S(2)}, u32[]{:S(2)}) %collective-permute-start.3) | collective-permute-done | bytes 262176 | tf_op jit(solution)/shard_map/ppermute | solution.py:21
  65.4 0.8 constant_dynamic-update-slice_fusion
  66.5 20.6 %collective-permute-done.4 = bf16[64,4096]{1,0:T(8,128)(2,1)S(1)} collective-permute-done((bf16[64,4096]{1,0:T(8,128)(2,1)S(1)}, bf16[64,4096]{1,0:T(8,128)(2,1)S(1)}, u32[]{:S(2)}, u32[]{:S(2)}) %collective-permute-start.4) | collective-permute-done | bytes 524320 | tf_op jit(solution)/shard_map/ppermute | solution.py:21
  87.1 0.8 constant_dynamic-update-slice_fusion.11
  87.9 0.6 constant_dynamic-update-slice_fusion.10
  88.5 0.6 constant_dynamic-update-slice_fusion.9
  89.1 0.6 constant_dynamic-update-slice_fusion.8
  89.8 0.7 constant_dynamic-update-slice_fusion.7
  90.4 0.7 constant_dynamic-update-slice_fusion.6
  91.2 0.9 constant_dynamic-update-slice_fusion.5
  92.0 11.8 %fusion = bf16[8192,1024]{0,1:T(8,128)(2,1)} fusion(bf16[8192,1024]{0,1:T(8,128)(2,1)} %copy.24, bf16[64,8192]{1,0:T(8,128)(2,1)} %all-gather.4.cloned.1.call-done, bf16[64,16384]{1,0:T(8,128)(2,1)} %constant_dynamic-update-slice_fusion.5, s32[]{:T(128)S(6)} %dynamic_slice.11), kind=kOutput, calls=%fused_computation.1 | convolution fusion | flops 1107296256 | bytes 34734084 | tf_op jit(solution)/shard_map/dot_general | solution.py:92
  103.9 9.1 %fusion.72 = f32[64,8,128]{2,0,1:T(8,128)S(1)} fusion(bf16[64,8192,1]{1,0,2:T(8,128)(2,1)} %bitcast.115, bf16[8,128,8192]{2,1,0:T(8,128)(2,1)} %bitcast.106), kind=kOutput, calls=%fused_computation.142 | convolution fusion | flops 1073741824 | bytes 18087936 | tf_op jit(solution)/shard_map/dot_general | solution.py:168
  113.1 0.4 maximum_bitcast_fusion
  113.9 1.3 fusion.71
  115.2 2.0 fusion.69
  117.4 1.3 fusion.67
  118.7 0.2 fusion.18
  118.9 0.7 fusion.16
  120.0 2.9 %fusion.22 = f32[16,8,128]{2,1,0:T(8,128)S(1)} fusion(bf16[16,1024,128]{2,1,0:T(8,128)(2,1)} %bitcast.111, f32[16,8,1024]{2,1,0:T(8,128)S(1)} %copy-done.3, f32[16,8]{1,0:T(8,128)S(1)} %add.119, f32[16,8]{1,0:T(8,128)S(1)} %max.31), kind=kOutput, calls=%fused_computation.45 | convolution fusion | flops 33947648 | bytes 4785152 | tf_op jit(solution)/shard_map/ngp,npd->ngd/dot_general | solution.py:82
  122.9 0.2 fusion.13
  123.2 0.2 fusion.20
  123.4 2.9 %fusion.23 = f32[16,8,128]{2,1,0:T(8,128)S(1)} fusion(bf16[16,1024,128]{2,1,0:T(8,128)(2,1)} %bitcast.112, f32[16,8,1024]{2,1,0:T(8,128)S(1)} %get-tuple-element.32, f32[16,8]{1,0:T(8,128)S(1)} %add.121, f32[16,8]{1,0:T(8,128)S(1)} %max.32), kind=kOutput, calls=%fused_computation.46 | convolution fusion | flops 33947648 | bytes 4785152 | tf_op jit(solution)/shard_map/ngp,npd->ngd/dot_general | solution.py:82
  126.4 0.2 fusion.14
  126.8 3.6 %fusion.65 = (f32[16,8]{1,0:T(8,128)S(1)}, f32[16,8,1024]{2,1,0:T(8,128)S(1)}) fusion(bf16[16,8,128]{2,1,0:T(8,128)(2,1)S(1)} %bitcast.121, bf16[16,1024,128]{2,1,0:T(8,128)(2,1)} %bitcast.107, pred[16,1024]{1,0:T(8,128)(4,1)S(1)} %iota_compare_fusion), kind=kOutput, calls=%fused_computation.135 | convolution fusion | flops 33947520 | bytes 4768256 | tf_op jit(solution)/shard_map/ngd,npd->ngp/dot_general | solution.py:63
  130.5 0.2 fusion.21
  130.8 0.7 fusion.24
  131.5 0.2 fusion.15
  131.8 55.2 %all-gather.8.cloned.1.call-done = bf16[64,8192]{1,0:T(8,128)(2,1)} async-done(((bf16[64,256]{1,0:T(8,128)(2,1)}), bf16[64,8192]{1,0:T(8,128)(2,1)}) %all-gather.8.cloned.1.call-update) | async-done | bytes 1048592 | tf_op jit(solution)/shard_map/all_gather | solution.py:123
  187.0 12.0 %fusion.5 = bf16[64,8192]{1,0:T(8,128)(2,1)} fusion(bf16[64,1024]{1,0:T(8,128)(2,1)S(1)} %bitcast.130, bf16[1024,8192]{1,0:T(8,128)(2,1)} %param.16, bf16[64,8192]{1,0:T(8,128)(2,1)} %all-gather.8.cloned.1.call-done, bf16[64,8192]{1,0:T(8,128)(2,1)} %all-gather.6.cloned.1.call-done, s32[]{:T(128)S(6)} %select_n.34), kind=kOutput, calls=%fused_computation.6 | convolution fusion | flops 2181562368 | bytes 19136516 | tf_op jit(solution)/shard_map/dot_general | solution.py:265
  199.0 35.8 %reduce-scatter.2.cloned.1.call-done = bf16[64,1024]{1,0:T(8,128)(2,1)} async-done(((bf16[64,8192]{1,0:T(8,128)(2,1)}), bf16[64,1024]{1,0:T(8,128)(2,1)}) %reduce-scatter.2.cloned.1.call-update) | async-done | bytes 131088 | tf_op jit(solution)/shard_map/reduce_scatter | solution.py:266
  (77 shorter events, 2.6 us)
Async XLA Ops:
  6.5 85.5 %all-gather.4.cloned.1.call-start = ((), (), s32[]{:S(2)}) async-start(), calls=%async_computation.1 | async-start | bytes 1081344 | tf_op jit(solution)/shard_map/all_gather | solution.py:122
  7.3 124.5 %all-gather.6.cloned.1.call-start = ((), (), s32[]{:S(2)}) async-start(), calls=%async_computation.2 | async-start | bytes 1081344 | tf_op jit(solution)/shard_map/all_gather | solution.py:125
  8.0 178.9 %all-gather.8.cloned.1.call-start = ((), (), s32[]{:S(2)}) async-start(), calls=%async_computation.3 | async-start | bytes 1081344 | tf_op jit(solution)/shard_map/all_gather | solution.py:123
  8.1 20.3 %collective-permute-start = (bf16[64,256]{1,0:T(8,128)(2,1)}, bf16[64,256]{1,0:T(8,128)(2,1)S(1)}, u32[]{:S(2)}, u32[]{:S(2)}) collective-permute-start(bf16[64,256]{1,0:T(8,128)(2,1)} %param.18), channel_id=1, source_target_pairs={{0,31},{1,0},{2,1},{3,2},{4,3},{5,4},{6,5},{7,6},{8,7},{9,8},{10,9... | collective-permute-start | bytes 98312 | tf_op jit(solution)/shard_map/ppermute | solution.py:21
  14.5 220.2 %reduce-scatter.2.cloned.1.call-start = ((), (), s32[]{:S(2)}) async-start(), calls=%async_computation.4 | async-start | bytes 1179648 | tf_op jit(solution)/shard_map/reduce_scatter | solution.py:266
  17.5 6.5 %copy-start.5 = (bf16[4,16,8192]{2,1,0:T(8,128)(2,1)S(1)}, bf16[4,16,8192]{2,1,0:T(8,128)(2,1)}, u32[]{:S(2)}) copy-start(bf16[4,16,8192]{2,1,0:T(8,128)(2,1)} %param.12) | copy-start | bytes 3145732
  24.3 8.5 %copy-start.4 = (bf16[4,16,8192]{2,1,0:T(8,128)(2,1)}, bf16[4,16,8192]{2,1,0:T(8,128)(2,1)S(1)}, u32[]{:S(2)}) copy-start(bf16[4,16,8192]{2,1,0:T(8,128)(2,1)S(1)} %fusion.8) | copy-start | bytes 3145732
  24.3 4.1 %copy-start.6 = (bf16[64,256]{1,0:T(8,128)(2,1)S(1)}, bf16[64,256]{1,0:T(8,128)(2,1)}, u32[]{:S(2)}) copy-start(bf16[64,256]{1,0:T(8,128)(2,1)} %param.18) | copy-start | bytes 98308
  24.3 5.6 %copy-start.7 = (s32[16]{0:T(128)S(1)}, s32[16]{0:T(128)}, u32[]{:S(2)}) copy-start(s32[16]{0:T(128)} %param.23) | copy-start | bytes 196
  28.4 4.3 %collective-permute-start.1 = (bf16[64,512]{1,0:T(8,128)(2,1)S(1)}, bf16[64,512]{1,0:T(8,128)(2,1)S(1)}, u32[]{:S(2)}, u32[]{:S(2)}) collective-permute-start(bf16[64,512]{1,0:T(8,128)(2,1)S(1)} %pad_maximum_fusion.3), channel_id=1, source_target_pairs={{0,30},{1,31},{2,0},{3,1},{4,2},{5,3},{6,4},{7,5},{8,6},{9,7},{10,... | collective-permute-start | bytes 196616 | tf_op jit(solution)/shard_map/ppermute | solution.py:21
  32.8 22.3 %collective-permute-start.2 = (bf16[64,1024]{1,0:T(8,128)(2,1)S(1)}, bf16[64,1024]{1,0:T(8,128)(2,1)S(1)}, u32[]{:S(2)}, u32[]{:S(2)}) collective-permute-start(bf16[64,1024]{1,0:T(8,128)(2,1)S(1)} %pad_maximum_fusion.1), channel_id=1, source_target_pairs={{0,28},{1,29},{2,30},{3,31},{4,0},{5,1},{6,2},{7,3},{8,4},{9,5},{1... | collective-permute-start | bytes 393224 | tf_op jit(solution)/shard_map/ppermute | solution.py:21
  55.1 10.3 %collective-permute-start.3 = (bf16[64,2048]{1,0:T(8,128)(2,1)S(1)}, bf16[64,2048]{1,0:T(8,128)(2,1)S(1)}, u32[]{:S(2)}, u32[]{:S(2)}) collective-permute-start(bf16[64,2048]{1,0:T(8,128)(2,1)S(1)} %pad_maximum_fusion), channel_id=1, source_target_pairs={{0,24},{1,25},{2,26},{3,27},{4,28},{5,29},{6,30},{7,31},{8,0},{9,1... | collective-permute-start | bytes 786440 | tf_op jit(solution)/shard_map/ppermute | solution.py:21
  66.2 20.9 %collective-permute-start.4 = (bf16[64,4096]{1,0:T(8,128)(2,1)S(1)}, bf16[64,4096]{1,0:T(8,128)(2,1)S(1)}, u32[]{:S(2)}, u32[]{:S(2)}) collective-permute-start(bf16[64,4096]{1,0:T(8,128)(2,1)S(1)} %get-tuple-element.7), channel_id=1, source_target_pairs={{0,16},{1,17},{2,18},{3,19},{4,20},{5,21},{6,22},{7,23},{8,24},{9,... | collective-permute-start | bytes 1572872 | tf_op jit(solution)/shard_map/ppermute | solution.py:21
  103.9 10.1 %copy-start = (bf16[2,8,1024,128]{3,2,1,0:T(8,128)(2,1)S(1)}, bf16[2,8,1024,128]{3,2,1,0:T(8,128)(2,1)}, u32[]{:S(2)}) copy-start(bf16[2,8,1024,128]{3,2,1,0:T(8,128)(2,1)} %param.21) | copy-start | bytes 12582916
  115.2 3.7 %copy-start.1 = (bf16[2,8,1024,128]{3,2,1,0:T(8,128)(2,1)S(1)}, bf16[2,8,1024,128]{3,2,1,0:T(8,128)(2,1)}, u32[]{:S(2)}) copy-start(bf16[2,8,1024,128]{3,2,1,0:T(8,128)(2,1)} %param.22) | copy-start | bytes 12582916
  118.7 1.1 copy-start.3
  126.6 4.1 %copy-start.2 = (bf16[2,8,1024,128]{3,2,1,0:T(8,128)(2,1)S(1)}, bf16[2,8,1024,128]{3,2,1,0:T(8,128)(2,1)}, u32[]{:S(2)}) copy-start(bf16[2,8,1024,128]{3,2,1,0:T(8,128)(2,1)} %param.22) | copy-start | bytes 12582916
Sparse Core Ops, SparseCore 0:
  10.2 56.3 all-gather.3
  69.4 62.2 all-gather.5
  134.6 52.2 all-gather.7
  199.1 35.6 reduce-scatter.1
